TPU v7x, 16 devices: a 4x2x1 block of a 4x4x8 slice. The times are simulated.
16 devices in a mesh: rep: 2 (over y, z), dp: 8 (over x, core).
Axes of the slice: x: 4, y: 2, z: 1, core: 2. Of those that a mesh axis runs over, the one named last changes fastest.
The devices are a block of a 4x4x8 slice.
Arguments:
- g_w_gate: bfloat16 [16, 2, 896, 2304], P(('rep', 'dp')), parts along dimension 0
- g_w_up: bfloat16 [16, 2, 896, 2304], P(('rep', 'dp')), parts along dimension 0
- g_w_down: bfloat16 [16, 2, 2304, 896], P(('rep', 'dp')), parts along dimension 0
- w_gate: bfloat16 [2, 896, 2304], replicated
- w_up: bfloat16 [2, 896, 2304], replicated
- w_down: bfloat16 [2, 2304, 896], replicated
- m_w_gate: float32 [2, 896, 2304], P(None, 'dp')
- m_w_up: float32 [2, 896, 2304], P(None, 'dp')
- m_w_down: float32 [2, 2304, 896], P(None, 'dp')
- v_w_gate: float32 [2, 896, 2304], P(None, 'dp')
- v_w_up: float32 [2, 896, 2304], P(None, 'dp')
- v_w_down: float32 [2, 2304, 896], P(None, 'dp')
Outputs:
- output 1: bfloat16 [4, 896, 2304], P('rep'), parts along dimension 0
- output 2: bfloat16 [4, 896, 2304], P('rep'), parts along dimension 0
- output 3: bfloat16 [4, 2304, 896], P('rep'), parts along dimension 0
- output 4: float32 [4, 896, 2304], P('rep', 'dp'), parts along dimension 0
- output 5: float32 [4, 896, 2304], P('rep', 'dp'), parts along dimension 0
- output 6: float32 [4, 2304, 896], P('rep', 'dp'), parts along dimension 0
- output 7: float32 [4, 896, 2304], P('rep', 'dp'), parts along dimension 0
- output 8: float32 [4, 896, 2304], P('rep', 'dp'), parts along dimension 0
- output 9: float32 [4, 2304, 896], P('rep', 'dp'), parts along dimension 0
There are 2 independent parts. A program takes and returns all parts, laid end to end along the dimension named above; an argument that names none is the same for every part.
All inputs are finite; a program needn't handle non-finite values.
Results may differ from a plain program's by a relative error of at most 0.022.
Values are sent between devices in bfloat16 or wider.
A program may use at most 768 MiB of HBM per device.

v0:
```python
import jax
import jax.numpy as jnp
from jax import lax
from jax.sharding import PartitionSpec as P


def adamw(w, m, v, g):
    m = 0.9 * m + 0.1 * g
    v = 0.95 * v + 0.05 * g * g
    step = m * lax.rsqrt(v + 1e-8) + 0.1 * w
    return (w - 0.02 * step).astype(jnp.bfloat16), m, v


def clipped(gradients, sum_of_squares, count):
    factor = jnp.minimum(1.0, 0.5 * lax.rsqrt(sum_of_squares / count + 1e-30))
    return [g * factor for g in gradients]


def solution(mesh):
    def step(*arrays):
        terms, weights, m, v = (arrays[i : i + 3] for i in (0, 3, 6, 9))
        gradients = [lax.psum_scatter(t[0], "dp", scatter_dimension=1, tiled=True).astype(jnp.float32) for t in terms]
        squares = lax.psum(sum(jnp.sum(g * g) for g in gradients), "dp")
        gradients = clipped(gradients, squares, lax.psum(1, "dp") * sum(g.size for g in gradients))
        me = lax.axis_index("dp")
        own = [lax.dynamic_slice_in_dim(w, me * one.shape[1], one.shape[1], 1).astype(jnp.float32) for w, one in zip(weights, m, strict=True)]
        new = [adamw(w, m, v, g) for w, m, v, g in zip(own, m, v, gradients, strict=True)]
        whole = [lax.all_gather(one[0], "dp", axis=1, tiled=True) for one in new]
        return (*whole, *(one[1] for one in new), *(one[2] for one in new))

    all_of, cut = P(None, None, None), P(None, "dp", None)
    return jax.shard_map(
        step,
        mesh=mesh,
        in_specs=(P(("rep", "dp"), None, None, None),) * 3 + (all_of,) * 3 + (cut,) * 6,
        out_specs=(P("rep", None, None),) * 3 + (P("rep", "dp", None),) * 6,
        check_vma=False,
    )
```

profile of v0, /device:TPU:113, one launch (start us, length us, event | category | flops | bytes accessed | tf_op | source)
XLA Modules:
  0.0 350.9 jit_solution(15568801542616035322)
XLA Ops:
  7.2 0.1 reduce-scatter.4.cloned.1.call-start
  7.3 0.7 reduce-scatter.4.cloned.1.call-update
  8.0 0.1 reduce-scatter.6.cloned.1.call-start
  8.1 0.7 reduce-scatter.6.cloned.1.call-update
  8.8 0.1 reduce-scatter.8.cloned.1.call-start
  8.9 0.7 reduce-scatter.8.cloned.1.call-update
  9.6 0.1 all-gather.8.cloned.1.call-start
  9.7 51.0 %reduce-scatter.4.cloned.1.call-done = bf16[2,112,2304]{2,1,0:T(8,128)(2,1)} async-done(((bf16[2,896,2304]{2,1,0:T(8,128)(2,1)}), bf16[2,112,2304]{2,1,0:T(8,128)(2,1)}) %reduce-scatter.4.cloned.1.call-update) | async-done | bytes 1032208 | tf_op jit(solution)/shard_map/reduce_scatter | solution.py:22
  60.6 2.4 fusion.9
  63.0 47.5 %reduce-scatter.6.cloned.1.call-done = bf16[2,112,2304]{2,1,0:T(8,128)(2,1)} async-done(((bf16[2,896,2304]{2,1,0:T(8,128)(2,1)}), bf16[2,112,2304]{2,1,0:T(8,128)(2,1)}) %reduce-scatter.6.cloned.1.call-update) | async-done | bytes 1032208 | tf_op jit(solution)/shard_map/reduce_scatter | solution.py:22
  110.5 2.4 fusion.10
  114.1 46.2 %reduce-scatter.8.cloned.1.call-done = bf16[2,288,896]{2,1,0:T(8,128)(2,1)} async-done(((bf16[2,2304,896]{2,1,0:T(8,128)(2,1)}), bf16[2,288,896]{2,1,0:T(8,128)(2,1)}) %reduce-scatter.8.cloned.1.call-update) | async-done | bytes 1032208 | tf_op jit(solution)/shard_map/reduce_scatter | solution.py:22
  160.3 2.4 fusion.11
  163.3 13.4 %psum.7 = f32[]{:T(128)} all-reduce(f32[]{:T(128)S(6)} %add.65), channel_id=1, replica_groups=mesh['rep'=2,'dp'=8] {'dp'}, use_global_device_ids=true, to_apply=%region_6.0 | all-reduce | flops 1 | bytes 8 | tf_op jit(solution)/shard_map/psum | solution.py:23
  177.4 0.0 copy-start.1
  177.4 5.9 %fusion.17 = (bf16[2,288,896]{2,1,0:T(8,128)(2,1)}, f32[2,288,896]{2,1,0:T(8,128)}, f32[2,288,896]{2,1,0:T(8,128)}) fusion(bf16[2,2304,896]{2,1,0:T(8,128)(2,1)} %param.17, s32[]{:T(128)S(6)} %select_n.8, f32[]{:T(128)S(6)} %min_shard_map.3, bf16[2,288,896]{2,1,0:T(8,128)(2,1)} %reduce-scatter.8.cloned.1.call-done, f32[2,288,896]{2,1,0:T(8,128)} %param.23, ...), kind=kLoop, calls=%fused_computation.32 | loop fusion | flops 8773632 | bytes 11354120 | tf_op jit(solution)/shard_map/convert_element_type | solution.py:11
  183.3 0.1 all-gather.8.cloned.1.call-update
  183.3 0.1 all-gather.4.cloned.1.call-start
  183.4 0.0 copy-done.1
  183.4 0.0 copy-start
  183.4 5.5 %fusion.8 = (bf16[2,112,2304]{2,1,0:T(8,128)(2,1)}, f32[2,112,2304]{2,1,0:T(8,128)}, f32[2,112,2304]{2,1,0:T(8,128)}) fusion(bf16[2,896,2304]{2,1,0:T(8,128)(2,1)} %param.15, s32[]{:T(128)S(6)} %select_n.7, f32[]{:T(128)S(6)} %min_shard_map.3, bf16[2,112,2304]{2,1,0:T(8,128)(2,1)S(1)} %copy-done.1, f32[2,112,2304]{2,1,0:T(8,128)} %param.21, ...), kind=kLoop, calls=%fused_computation.23 | loop fusion | flops 8773632 | bytes 11354120 | tf_op jit(solution)/shard_map/convert_element_type | solution.py:11
  188.9 0.1 all-gather.4.cloned.1.call-update
  188.9 0.1 all-gather.6.cloned.1.call-start
  189.0 0.0 copy-done
  189.0 5.4 %fusion.14 = (bf16[2,112,2304]{2,1,0:T(8,128)(2,1)}, f32[2,112,2304]{2,1,0:T(8,128)}, f32[2,112,2304]{2,1,0:T(8,128)}) fusion(bf16[2,896,2304]{2,1,0:T(8,128)(2,1)} %param.16, s32[]{:T(128)S(6)} %select_n.7, f32[]{:T(128)S(6)} %min_shard_map.3, bf16[2,112,2304]{2,1,0:T(8,128)(2,1)S(1)} %copy-done, f32[2,112,2304]{2,1,0:T(8,128)} %param.22, ...), kind=kLoop, calls=%fused_computation.29 | loop fusion | flops 8773632 | bytes 11354120 | tf_op jit(solution)/shard_map/convert_element_type | solution.py:11
  194.4 0.1 all-gather.6.cloned.1.call-update
  194.5 33.5 %all-gather.8.cloned.1.call-done = bf16[2,2304,896]{2,1,0:T(8,128)(2,1)} async-done(((bf16[2,288,896]{2,1,0:T(8,128)(2,1)}), bf16[2,2304,896]{2,1,0:T(8,128)(2,1)}) %all-gather.8.cloned.1.call-update) | async-done | bytes 8257552 | tf_op jit(solution)/shard_map/all_gather | solution.py:28
  228.0 47.1 %all-gather.4.cloned.1.call-done = bf16[2,896,2304]{2,1,0:T(8,128)(2,1)} async-done(((bf16[2,112,2304]{2,1,0:T(8,128)(2,1)}), bf16[2,896,2304]{2,1,0:T(8,128)(2,1)}) %all-gather.4.cloned.1.call-update) | async-done | bytes 8257552 | tf_op jit(solution)/shard_map/all_gather | solution.py:28
  275.1 47.1 %all-gather.6.cloned.1.call-done = bf16[2,896,2304]{2,1,0:T(8,128)(2,1)} async-done(((bf16[2,112,2304]{2,1,0:T(8,128)(2,1)}), bf16[2,896,2304]{2,1,0:T(8,128)(2,1)}) %all-gather.6.cloned.1.call-update) | async-done | bytes 8257552 | tf_op jit(solution)/shard_map/all_gather | solution.py:28
  322.3 7.2 %copy.24 = bf16[2,896,2304]{2,1,0:T(8,128)(2,1)} copy(bf16[2,896,2304]{2,1,0:T(8,128)(2,1)} %all-gather.4.cloned.1.call-done) | data formatting | bytes 16515072
  329.5 7.2 %copy.25 = bf16[2,896,2304]{2,1,0:T(8,128)(2,1)} copy(bf16[2,896,2304]{2,1,0:T(8,128)(2,1)} %all-gather.6.cloned.1.call-done) | data formatting | bytes 16515072
  336.7 7.3 %copy.26 = bf16[2,2304,896]{2,1,0:T(8,128)(2,1)} copy(bf16[2,2304,896]{2,1,0:T(8,128)(2,1)} %all-gather.8.cloned.1.call-done) | data formatting | bytes 16515072
Async XLA Ops:
  7.2 53.4 %reduce-scatter.4.cloned.1.call-start = ((), (), s32[]{:S(2)}) async-start(), calls=%async_computation.3 | async-start | bytes 9289728 | tf_op jit(solution)/shard_map/reduce_scatter | solution.py:22
  8.0 102.5 %reduce-scatter.6.cloned.1.call-start = ((), (), s32[]{:S(2)}) async-start(), calls=%async_computation.4 | async-start | bytes 9289728 | tf_op jit(solution)/shard_map/reduce_scatter | solution.py:22
  8.8 151.5 %reduce-scatter.8.cloned.1.call-start = ((), (), s32[]{:S(2)}) async-start(), calls=%async_computation.5 | async-start | bytes 9289728 | tf_op jit(solution)/shard_map/reduce_scatter | solution.py:22
  9.6 218.4 %all-gather.8.cloned.1.call-start = ((), (), s32[]{:S(2)}) async-start(), calls=%async_computation.8 | async-start | bytes 9289728 | tf_op jit(solution)/shard_map/all_gather | solution.py:28
  177.4 6.0 %copy-start.1 = (bf16[2,112,2304]{2,1,0:T(8,128)(2,1)S(1)}, bf16[2,112,2304]{2,1,0:T(8,128)(2,1)}, u32[]{:S(2)}) copy-start(bf16[2,112,2304]{2,1,0:T(8,128)(2,1)} %reduce-scatter.4.cloned.1.call-done) | copy-start | bytes 3096580
  183.3 91.8 %all-gather.4.cloned.1.call-start = ((), (), s32[]{:S(2)}) async-start(), calls=%async_computation.6 | async-start | bytes 9289728 | tf_op jit(solution)/shard_map/all_gather | solution.py:28
  183.4 5.6 %copy-start = (bf16[2,112,2304]{2,1,0:T(8,128)(2,1)S(1)}, bf16[2,112,2304]{2,1,0:T(8,128)(2,1)}, u32[]{:S(2)}) copy-start(bf16[2,112,2304]{2,1,0:T(8,128)(2,1)} %reduce-scatter.6.cloned.1.call-done) | copy-start | bytes 3096580
  188.9 133.3 %all-gather.6.cloned.1.call-start = ((), (), s32[]{:S(2)}) async-start(), calls=%async_computation.7 | async-start | bytes 9289728 | tf_op jit(solution)/shard_map/all_gather | solution.py:28
Sparse Core Ops, SparseCore 0:
  10.3 50.2 reduce-scatter.3
  63.0 47.4 reduce-scatter.5
  112.8 47.4 reduce-scatter.7
  183.4 44.5 all-gather.7
  230.0 45.0 all-gather.3
  277.1 45.0 all-gather.5
where the time goes:
time: 351 us
  waiting for transfers between devices  275 us (78%)
  other arithmetic  23.8 us (7%)
  local copies, waits for them, and re-layouts  21.8 us (6%)
  between operations  16.8 us (5%)
  blocking collectives  13.4 us (4%)
    reduce_scatter x3, waiting for transfers between devices, step(): lax.psum_scatter(t[0], 'dp', scatter_dimension=1, tiled=True)  145 us
    all_gather x3, waiting for transfers between devices, step(): whole = [lax.all_gather(one[0], 'dp', axis=1, tiled=True) for one in new]  128 us
    unnamed x7, local copies, waits for them, and re-layouts  21.8 us
    convert_element_type x3, other arithmetic, adamw(): return ((w - 0.02 * step).astype(jnp.bfloat16), m, v)  16.7 us
    psum x1, blocking collectives, step(): squares = lax.psum(sum((jnp.sum(g * g) for g in gradients)), 'dp')  13.4 us
    reduce_sum x3, other arithmetic, step(): squares = lax.psum(sum((jnp.sum(g * g) for g in gradients)), 'dp')  7.06 us
  transfers between devices with their start and end apart: 6, of which 6 were waited for; matrix products, arithmetic and copies ran while one was open for 4% of the time, Pallas kernels for 0%

commit v1 on v0

v1 whole, which is shorter than its diff:
```python
import functools

import jax
import jax.numpy as jnp
from jax import lax
from jax.experimental import pallas as pl
from jax.experimental.pallas import tpu as pltpu
from jax.sharding import PartitionSpec as P

LAYERS = 2
KINDS = 3
MESH = pl.DeviceIdType.MESH


def strip(columns):
    return 16 if columns > 1024 else 48


def tile_sum(x):
    tiles = [x[r : r + 8, c : c + 128] for r in range(0, x.shape[0], 8) for c in range(0, x.shape[1], 128)]
    while len(tiles) > 1:
        tiles = [a + b for a, b in zip(tiles[::2], tiles[1::2])] + ([tiles[-1]] if len(tiles) % 2 else [])
    return tiles[0]


def kernel(size, count, *refs):
    chips = size // 2
    take = iter(refs)
    some = lambda n: [next(take) for _ in range(n)]
    g_in, w_in, m_in, v_in = some(KINDS), some(KINDS), some(KINDS), some(KINDS)
    W, M, V = some(KINDS), some(KINDS), some(KINDS)
    old, hop, last = some(KINDS), some(KINDS), some(KINDS)
    squares, own_sem, load_sem, peer_send, peer_recv, link_send, link_recv, sq_send, sq_recv = some(9)

    me = lax.axis_index("dp")
    chip, core = me // 2, lax.rem(me, 2)
    at = lambda offset: lax.rem(chip + offset, chips)
    sibling = chip * 2 + 1 - core
    ahead, behind = at(1) * 2 + core, at(chips - 1) * 2 + core
    across = chips // 2
    offsets = (across, 1, chips - 1, 0)
    rows = [m.shape[1] for m in m_in]

    def block(a, device, start=0, height=None):
        return pl.ds(pl.multiple_of(device * rows[a] + start, 16), rows[a] if height is None else height)

    def unit(o, l, a):
        return (offsets.index(o) * LAYERS + l) * KINDS + a

    def mine(o):
        return at(o) * 2 + core

    def theirs(o):
        return at(o) * 2 + 1 - core

    own = {}
    for o in offsets:
        for a in range(KINDS):
            for l in range(LAYERS):
                place = W[a].at[l, block(a, mine(o))]
                own[o, l, a] = pltpu.make_async_copy(g_in[a].at[0, l, block(a, mine(o))], place, own_sem.at[unit(o, l, a)])
                own[o, l, a].start()

    barrier = pltpu.get_barrier_semaphore()
    for step in range(1, size):
        pl.semaphore_signal(barrier, inc=1, device_id={"dp": lax.rem(me + step, size)}, device_id_type=MESH)
    pl.semaphore_wait(barrier, size - 1)

    given = {}
    for o in offsets:
        for a in range(KINDS):
            for l in range(LAYERS):
                given[o, l, a] = pltpu.make_async_remote_copy(
                    g_in[a].at[0, l, block(a, theirs(o))],
                    W[a].at[l, block(a, mine(o))],
                    peer_send.at[unit(o, l, a)],
                    peer_recv.at[unit(o, l, a)],
                    device_id={"dp": sibling},
                    device_id_type=MESH,
                )
                given[o, l, a].start()

    loads = []
    for l in range(LAYERS):
        for a in range(KINDS):
            for n, (source, target) in enumerate(
                ((w_in[a].at[l, block(a, me)], old[a].at[l]), (m_in[a].at[l], M[a].at[l]), (v_in[a].at[l], V[a].at[l]))
            ):
                loads.append(pltpu.make_async_copy(source, target, load_sem.at[(l * KINDS + a) * 3 + n]))
                loads[-1].start()

    def each_strip(a, body, init):
        height = strip(g_in[a].shape[-1])
        return lax.fori_loop(0, rows[a] // height, lambda i, carry: body(pl.multiple_of(i * height, 16), height, carry), init)

    def add(o, l, a, more=()):
        own[o, l, a].wait()
        given[o, l, a].wait_recv()

        def body(start, height, carry):
            here = W[a].at[l, block(a, mine(o), start, height)]
            total = here[...].astype(jnp.float32) + W[a][l, block(a, theirs(o), start, height)].astype(jnp.float32)
            for other in more:
                total = total + other[pl.ds(start, height)].astype(jnp.float32)
            total = total.astype(jnp.bfloat16)
            here[...] = total
            if o == 0:
                total = total.astype(jnp.float32)
                carry = carry + tile_sum(total * total)
            return carry

        return each_strip(a, body, jnp.zeros((8, 128), jnp.float32) if o == 0 else 0)

    def to_link(source, target, slot, device):
        copy = pltpu.make_async_remote_copy(
            source, target, link_send.at[slot], link_recv.at[slot], device_id={"dp": device}, device_id_type=MESH
        )
        copy.start()
        return copy

    side = lambda forward: 0 if forward else 1
    slot = lambda forward, stage, a: (side(forward) * 3 + stage) * KINDS + a
    sent = {}
    for a in range(KINDS):
        for forward, l in ((True, 0), (False, 1)):
            add(across, l, a)
            sent[forward, 0, a] = to_link(
                W[a].at[l, block(a, mine(across))], hop[a].at[l], slot(forward, 0, a), ahead if forward else behind
            )
    for a in range(KINDS):
        for forward, l in ((True, 1), (False, 0)):
            o = 1 if forward else chips - 1
            add(o, l, a)
            sent[forward, 1, a] = to_link(
                W[a].at[l, block(a, mine(o))], last[a].at[side(forward), l], slot(forward, 1, a), ahead if forward else behind
            )
    for a in range(KINDS):
        for forward, l in ((True, 0), (False, 1)):
            o = 1 if forward else chips - 1
            sent[forward, 0, a].wait_recv()
            add(o, l, a, (hop[a].at[l],))
            sent[forward, 2, a] = to_link(
                W[a].at[l, block(a, mine(o))], last[a].at[side(forward), l], slot(forward, 2, a), ahead if forward else behind
            )
    total = jnp.zeros((8, 128), jnp.float32)
    for a in range(KINDS):
        for l in range(LAYERS):
            sent[True, 2 - l, a].wait_recv()
            sent[False, 1 + l, a].wait_recv()
            total = total + add(0, l, a, (last[a].at[0, l], last[a].at[1, l]))
    for copy in (*given.values(), *sent.values()):
        copy.wait_send()

    squares[me] = total
    told = []
    for step in range(1, size):
        told.append(
            pltpu.make_async_remote_copy(
                squares.at[me],
                squares.at[me],
                sq_send.at[step - 1],
                sq_recv.at[step - 1],
                device_id={"dp": lax.rem(me + step, size)},
                device_id_type=MESH,
            )
        )
        told[-1].start()
    for copy in loads:
        copy.wait()
    for copy in told:
        copy.wait_recv()
    everything = jnp.sum(jnp.sum(squares[...], axis=0), keepdims=True)
    factor = jnp.minimum(1.0, 0.5 * lax.rsqrt(everything / count + 1e-30))

    def update(l, a):
        def body(start, height, carry):
            here = W[a].at[l, block(a, me, start, height)]
            part = pl.ds(start, height)
            g = here[...].astype(jnp.float32) * factor
            w = old[a][l, part].astype(jnp.float32)
            m = 0.9 * M[a][l, part] + 0.1 * g
            v = 0.95 * V[a][l, part] + 0.05 * g * g
            M[a][l, part] = m
            V[a][l, part] = v
            here[...] = (w - 0.02 * (m * lax.rsqrt(v + 1e-8) + 0.1 * w)).astype(jnp.bfloat16)
            return carry

        each_strip(a, body, 0)

    def share(o, l, a):
        place = W[a].at[l, block(a, mine(o))]
        copy = pltpu.make_async_remote_copy(
            place, place, peer_send.at[unit(o, l, a)], peer_recv.at[unit(o, l, a)], device_id={"dp": sibling}, device_id_type=MESH
        )
        copy.start()
        return copy

    def pass_on(forward, stage, o, l, a):
        place = W[a].at[l, block(a, mine(o))]
        sent[forward, stage, a] = to_link(place, place, slot(forward, stage, a), ahead if forward else behind)

    shared = []
    for a in range(KINDS):
        for forward, l in ((True, 0), (False, 1)):
            update(l, a)
            pass_on(forward, 0, 0, l, a)
            shared.append(share(0, l, a))
    for a in range(KINDS):
        for forward, l in ((True, 1), (False, 0)):
            pass_on(forward, 1, 0, l, a)
    for stage in range(3):
        for a in range(KINDS):
            for forward, l in ((True, 0), (False, 1)):
                l = 1 - l if stage == 1 else l
                sent[forward, stage, a].wait_recv()
                o = across if stage == 2 else chips - 1 if forward else 1
                if stage == 0:
                    pass_on(forward, 2, o, l, a)
                shared.append(share(o, l, a))
    for copy in shared:
        copy.wait_recv()
    for copy in (*shared, *sent.values(), *told):
        copy.wait_send()


def put_out(*refs):
    *refs, sems = refs
    n = len(refs) // 2
    copies = [pltpu.make_async_copy(a, b, sems.at[i]) for i, (a, b) in enumerate(zip(refs[:n], refs[n:]))]
    for copy in copies:
        copy.start()
    for copy in copies:
        copy.wait()


def solution(mesh):
    size = mesh.shape["dp"]

    def step(*arrays):
        terms, weights, m, v = (arrays[i : i + 3] for i in (0, 3, 6, 9))
        count = size * sum(one.size for one in m)
        in_vmem = [pltpu.VMEM(x.shape, x.dtype) for x in (*weights, *m, *v)]
        blocks = [(LAYERS, *one.shape[1:]) for one in m]
        dma = lambda n: pltpu.SemaphoreType.DMA((n,))
        units = 4 * LAYERS * KINDS
        out = pl.pallas_call(
            functools.partial(kernel, size, count),
            out_shape=in_vmem,
            in_specs=[pl.BlockSpec(memory_space=pltpu.HBM)] * 12,
            out_specs=[pl.BlockSpec(memory_space=pltpu.VMEM)] * 9,
            scratch_shapes=[
                *(pltpu.VMEM(b, jnp.bfloat16) for b in blocks),
                *(pltpu.VMEM(b, jnp.bfloat16) for b in blocks),
                *(pltpu.VMEM((2, *b), jnp.bfloat16) for b in blocks),
                pltpu.VMEM((size, 8, 128), jnp.float32),
                dma(units),
                dma(18),
                dma(units),
                dma(units),
                dma(18),
                dma(18),
                dma(size - 1),
                dma(size - 1),
            ],
            compiler_params=pltpu.CompilerParams(
                collective_id=0, has_side_effects=True, vmem_limit_bytes=16 << 20
            ),
            name="step",
        )(*(pltpu.with_memory_space_constraint(x, pltpu.HBM) for x in arrays))
        return pl.pallas_call(
            put_out,
            out_shape=[jax.ShapeDtypeStruct(x.shape, x.dtype) for x in out],
            in_specs=[pl.BlockSpec(memory_space=pltpu.VMEM)] * 9,
            out_specs=[pl.BlockSpec(memory_space=pltpu.HBM)] * 9,
            scratch_shapes=[dma(9)],
            compiler_params=pltpu.CompilerParams(vmem_limit_bytes=16 << 20),
            name="put_out",
        )(*(x for x in out))

    all_of, cut = P(None, None, None), P(None, "dp", None)
    return jax.shard_map(
        step,
        mesh=mesh,
        in_specs=(P(("rep", "dp"), None, None, None),) * 3 + (all_of,) * 3 + (cut,) * 6,
        out_specs=(P("rep", None, None),) * 3 + (P("rep", "dp", None),) * 6,
        check_vma=False,
    )
```

time: 351 us -> 232 us (0.66)
  waiting for transfers between devices: 275 us -> 0 us
  Pallas kernels: 0 us -> 232 us
  other arithmetic: 23.8 us -> 0 us
  local copies, waits for them, and re-layouts: 21.8 us -> 0 us
  between operations: 16.8 us -> 0.65 us
  blocking collectives: 13.4 us -> 0 us
    pallas_call x0 -> x2, Pallas kernels: none -> 232 us  [the longest x1 219 us: step(): pl.pallas_call(functools.partial(kernel, size, count), out_shape=in_vmem,...]
    reduce_scatter x3 -> x0, waiting for transfers between devices: 145 us -> none  [step(): lax.psum_scatter(t[0], 'dp', scatter_dimension=1, tiled=True)]
    all_gather x3 -> x0, waiting for transfers between devices: 128 us -> none  [step(): whole = [lax.all_gather(one[0], 'dp', axis=1, tiled=True) for one in new]]
    unnamed x7 -> x0, local copies, waits for them, and re-layouts: 21.8 us -> none
    convert_element_type x3 -> x0, other arithmetic: 16.7 us -> none  [adamw(): return ((w - 0.02 * step).astype(jnp.bfloat16), m, v)]
    psum x1 -> x0, blocking collectives: 13.4 us -> none  [step(): squares = lax.psum(sum((jnp.sum(g * g) for g in gradients)), 'dp')]
    reduce_sum x3 -> x0, other arithmetic: 7.06 us -> none  [step(): squares = lax.psum(sum((jnp.sum(g * g) for g in gradients)), 'dp')]
  transfers between devices with their start and end apart: 6 -> 0, of which waited for: 6 -> 0; matrix products, arithmetic and copies ran while one was open for 4% -> 0% of each run, Pallas kernels for 0% -> 0%
where the time goes in v1:
time: 232 us
  Pallas kernels  232 us (100%)
    pallas_call x1, Pallas kernels, step(): pl.pallas_call(functools.partial(kernel, size, count), out_shape=in_vmem,...  219 us
    pallas_call x1, Pallas kernels, step(): pl.pallas_call(put_out, out_shape=[jax.ShapeDtypeStruct(x.shape, x.dtype)...  12.2 us

profile of v1, /device:TPU:113, one launch (start us, length us, event | category | flops | bytes accessed | tf_op | source)
XLA Modules:
  0.0 232.3 jit_solution(14249830815348385826)
XLA Ops:
  0.6 219.4 %step.1 = (bf16[2,896,2304]{2,1,0:T(8,128)(2,1)S(1)}, bf16[2,896,2304]{2,1,0:T(8,128)(2,1)S(1)}, bf16[2,2304,896]{2,1,0:T(8,128)(2,1)S(1)}, f32[2,112,2304]{2,1,...) custom-call(bf16[1,2,896,2304]{3,2,1,0:T(8,128)(2,1)} %refs_0_.1, ...), custom_call_target="tpu_custom_call" | custom-call | tf_op jit(solution)/shard_map/step/pallas_call | solution.py:246
  220.1 12.2 %put_out.1 = (bf16[2,896,2304]{2,1,0:T(8,128)(2,1)}, bf16[2,896,2304]{2,1,0:T(8,128)(2,1)}, bf16[2,2304,896]{2,1,0:T(8,128)(2,1)}, f32[2,112,2304]{2,1,0:T(8,128...) custom-call(bf16[2,896,2304]{2,1,0:T(8,128)(2,1)S(1)} %get-tuple-ele, ...), custom_call_target="tpu_custom_call" | custom-call | tf_op jit(solution)/shard_map/put_out/pallas_call | solution.py:270

commit v2 on v1

v2 whole, which is shorter than its diff:
```python
import functools

import jax
import jax.numpy as jnp
from jax import lax
from jax.experimental import pallas as pl
from jax.experimental.pallas import tpu as pltpu
from jax.sharding import PartitionSpec as P

LAYERS = 2
KINDS = 3
MESH = pl.DeviceIdType.MESH


def strip(columns):
    return 16 if columns > 1024 else 48


def tile_sum(x):
    tiles = [x[r : r + 8, c : c + 128] for r in range(0, x.shape[0], 8) for c in range(0, x.shape[1], 128)]
    while len(tiles) > 1:
        tiles = [a + b for a, b in zip(tiles[::2], tiles[1::2])] + ([tiles[-1]] if len(tiles) % 2 else [])
    return tiles[0]


def cut(rows, columns):
    pieces = []
    for a in range(KINDS):
        small = strip(columns[a])
        heights = [small, rows[a] - small] if a == 0 else [rows[a]] if a < KINDS - 1 else [rows[a] - small, small]
        pieces += [(a, sum(heights[:i]), h) for i, h in enumerate(heights)]
    return pieces


def kernel(size, count, pieces, *refs):
    chips = size // 2
    take = iter(refs)
    some = lambda n: [next(take) for _ in range(n)]
    g_in, w_in, m_in, v_in = some(KINDS), some(KINDS), some(KINDS), some(KINDS)
    W, M, V = some(KINDS), some(KINDS), some(KINDS)
    old, hop, last = some(KINDS), some(KINDS), some(KINDS)
    squares, own_sem, load_sem, peer_send, peer_recv, link_send, link_recv, sq_send, sq_recv = some(9)

    me = lax.axis_index("dp")
    chip, core = me // 2, lax.rem(me, 2)
    at = lambda offset: lax.rem(chip + offset, chips)
    sibling = chip * 2 + 1 - core
    ahead, behind = at(1) * 2 + core, at(chips - 1) * 2 + core
    across = chips // 2
    offsets = (across, 1, chips - 1, 0)
    rows = [m.shape[1] for m in m_in]
    every = range(len(pieces))

    barrier = pltpu.get_barrier_semaphore()
    for step in range(1, size):
        pl.semaphore_signal(barrier, inc=1, device_id={"dp": lax.rem(me + step, size)}, device_id_type=MESH)

    def block(q, device, start=None, height=None):
        a, first, high = pieces[q]
        start, height = (first, high) if start is None else (start, height)
        return pl.ds(pl.multiple_of(device * rows[a] + start, 16), height)

    def part(q):
        return pl.ds(pieces[q][1], pieces[q][2])

    def unit(o, l, q):
        return (offsets.index(o) * LAYERS + l) * len(pieces) + q

    def mine(o):
        return at(o) * 2 + core

    def theirs(o):
        return at(o) * 2 + 1 - core

    own, given = {}, {}

    def fetch(o):
        for q in every:
            for l in range(LAYERS):
                a, here = pieces[q][0], block(q, mine(o))
                own[o, l, q] = pltpu.make_async_copy(g_in[a].at[0, l, here], W[a].at[l, here], own_sem.at[unit(o, l, q)])
                own[o, l, q].start()

    def give(o):
        for q in every:
            for l in range(LAYERS):
                a = pieces[q][0]
                given[o, l, q] = pltpu.make_async_remote_copy(
                    g_in[a].at[0, l, block(q, theirs(o))],
                    W[a].at[l, block(q, mine(o))],
                    peer_send.at[unit(o, l, q)],
                    peer_recv.at[unit(o, l, q)],
                    device_id={"dp": sibling},
                    device_id_type=MESH,
                )
                given[o, l, q].start()

    def each_strip(q, body, init):
        a, first, high = pieces[q]
        height = strip(g_in[a].shape[-1])
        if high == height:
            return body(first, height, init)
        return lax.fori_loop(
            0, high // height, lambda i, carry: body(pl.multiple_of(first + i * height, 16), height, carry), init
        )

    def add(o, l, q, more=()):
        own[o, l, q].wait()
        given[o, l, q].wait_recv()
        a = pieces[q][0]

        def body(start, height, carry):
            here = W[a].at[l, block(q, mine(o), start, height)]
            total = here[...].astype(jnp.float32) + W[a][l, block(q, theirs(o), start, height)].astype(jnp.float32)
            for other in more:
                total = total + other[pl.ds(start, height)].astype(jnp.float32)
            total = total.astype(jnp.bfloat16)
            here[...] = total
            if o == 0:
                total = total.astype(jnp.float32)
                carry = carry + tile_sum(total * total)
            return carry

        return each_strip(q, body, jnp.zeros((8, 128), jnp.float32) if o == 0 else 0)

    sent = {}

    def to_link(forward, stage, q, source, target):
        slot = ((0 if forward else 1) * 3 + stage) * len(pieces) + q
        sent[forward, stage, q] = pltpu.make_async_remote_copy(
            source,
            target,
            link_send.at[slot],
            link_recv.at[slot],
            device_id={"dp": ahead if forward else behind},
            device_id_type=MESH,
        )
        sent[forward, stage, q].start()

    fetch(across)
    pl.semaphore_wait(barrier, size - 1)
    give(across)
    for o in (1, chips - 1):
        fetch(o)
        give(o)
    for q in every:
        for forward, l in ((True, 0), (False, 1)):
            add(across, l, q)
            a = pieces[q][0]
            to_link(forward, 0, q, W[a].at[l, block(q, mine(across))], hop[a].at[l, part(q)])
    fetch(0)
    give(0)
    for q in every:
        for forward, l in ((True, 1), (False, 0)):
            o = 1 if forward else chips - 1
            add(o, l, q)
            a = pieces[q][0]
            to_link(forward, 1, q, W[a].at[l, block(q, mine(o))], last[a].at[0 if forward else 1, l, part(q)])
    loads = []
    for l in range(LAYERS):
        for a in range(KINDS):
            its = pl.ds(pl.multiple_of(me * rows[a], 16), rows[a])
            for n, (source, target) in enumerate(
                ((w_in[a].at[l, its], old[a].at[l]), (m_in[a].at[l], M[a].at[l]), (v_in[a].at[l], V[a].at[l]))
            ):
                loads.append(pltpu.make_async_copy(source, target, load_sem.at[(l * KINDS + a) * 3 + n]))
                loads[-1].start()
    for q in every:
        for forward, l in ((True, 0), (False, 1)):
            o = 1 if forward else chips - 1
            sent[forward, 0, q].wait_recv()
            a = pieces[q][0]
            add(o, l, q, (hop[a].at[l],))
            to_link(forward, 2, q, W[a].at[l, block(q, mine(o))], last[a].at[0 if forward else 1, l, part(q)])
    for copy in loads:
        copy.wait()
    total = jnp.zeros((8, 128), jnp.float32)
    for q in every:
        for l in range(LAYERS):
            sent[True, 2 - l, q].wait_recv()
            sent[False, 1 + l, q].wait_recv()
            a = pieces[q][0]
            total = total + add(0, l, q, (last[a].at[0, l], last[a].at[1, l]))
    for copy in (*given.values(), *sent.values()):
        copy.wait_send()

    squares[me] = total
    told = []
    for step in range(1, size):
        told.append(
            pltpu.make_async_remote_copy(
                squares.at[me],
                squares.at[me],
                sq_send.at[step - 1],
                sq_recv.at[step - 1],
                device_id={"dp": lax.rem(me + step, size)},
                device_id_type=MESH,
            )
        )
        told[-1].start()
    for copy in told:
        copy.wait_recv()
    everything = jnp.sum(jnp.sum(squares[...], axis=0), keepdims=True)
    factor = jnp.minimum(1.0, 0.5 * lax.rsqrt(everything / count + 1e-30))

    def update(l, q):
        a = pieces[q][0]

        def body(start, height, carry):
            here = W[a].at[l, block(q, me, start, height)]
            its = pl.ds(start, height)
            g = here[...].astype(jnp.float32) * factor
            w = old[a][l, its].astype(jnp.float32)
            m = 0.9 * M[a][l, its] + 0.1 * g
            v = 0.95 * V[a][l, its] + 0.05 * g * g
            M[a][l, its] = m
            V[a][l, its] = v
            here[...] = (w - 0.02 * (m * lax.rsqrt(v + 1e-8) + 0.1 * w)).astype(jnp.bfloat16)
            return carry

        each_strip(q, body, 0)

    shared = []

    def share(o, l, q):
        place = W[pieces[q][0]].at[l, block(q, mine(o))]
        u = unit(o, l, q)
        shared.append(
            pltpu.make_async_remote_copy(
                place, place, peer_send.at[u], peer_recv.at[u], device_id={"dp": sibling}, device_id_type=MESH
            )
        )
        shared[-1].start()

    def pass_on(forward, stage, o, l, q):
        place = W[pieces[q][0]].at[l, block(q, mine(o))]
        to_link(forward, stage, q, place, place)

    for q in every:
        for forward, l in ((True, 0), (False, 1)):
            update(l, q)
            pass_on(forward, 0, 0, l, q)
    for q in every:
        for forward, l in ((True, 1), (False, 0)):
            pass_on(forward, 1, 0, l, q)
            share(0, l, q)
    for stage in range(3):
        for q in every:
            for forward, l in ((True, 0), (False, 1)):
                l = 1 - l if stage == 1 else l
                sent[forward, stage, q].wait_recv()
                o = across if stage == 2 else chips - 1 if forward else 1
                if stage == 0:
                    pass_on(forward, 2, o, l, q)
                share(o, l, q)
    for copy in shared:
        copy.wait_recv()
    for copy in (*shared, *sent.values(), *told):
        copy.wait_send()


def put_out(*refs):
    *refs, sems = refs
    n = len(refs) // 2
    copies = [pltpu.make_async_copy(a, b, sems.at[i]) for i, (a, b) in enumerate(zip(refs[:n], refs[n:]))]
    for copy in copies:
        copy.start()
    for copy in copies:
        copy.wait()


def solution(mesh):
    size = mesh.shape["dp"]

    def step(*arrays):
        terms, weights, m, v = (arrays[i : i + 3] for i in (0, 3, 6, 9))
        count = size * sum(one.size for one in m)
        in_vmem = [pltpu.VMEM(x.shape, x.dtype) for x in (*weights, *m, *v)]
        blocks = [(LAYERS, *one.shape[1:]) for one in m]
        dma = lambda n: pltpu.SemaphoreType.DMA((n,))
        pieces = cut([one.shape[1] for one in m], [one.shape[2] for one in m])
        units, hops = 4 * LAYERS * len(pieces), 6 * len(pieces)
        out = pl.pallas_call(
            functools.partial(kernel, size, count, pieces),
            out_shape=in_vmem,
            in_specs=[pl.BlockSpec(memory_space=pltpu.HBM)] * 12,
            out_specs=[pl.BlockSpec(memory_space=pltpu.VMEM)] * 9,
            scratch_shapes=[
                *(pltpu.VMEM(b, jnp.bfloat16) for b in blocks),
                *(pltpu.VMEM(b, jnp.bfloat16) for b in blocks),
                *(pltpu.VMEM((2, *b), jnp.bfloat16) for b in blocks),
                pltpu.VMEM((size, 8, 128), jnp.float32),
                dma(units),
                dma(3 * LAYERS * KINDS),
                dma(units),
                dma(units),
                dma(hops),
                dma(hops),
                dma(size - 1),
                dma(size - 1),
            ],
            compiler_params=pltpu.CompilerParams(
                collective_id=0, has_side_effects=True, vmem_limit_bytes=16 << 20
            ),
            name="step",
        )(*(pltpu.with_memory_space_constraint(x, pltpu.HBM) for x in arrays))
        return pl.pallas_call(
            put_out,
            out_shape=[jax.ShapeDtypeStruct(x.shape, x.dtype) for x in out],
            in_specs=[pl.BlockSpec(memory_space=pltpu.VMEM)] * 9,
            out_specs=[pl.BlockSpec(memory_space=pltpu.HBM)] * 9,
            scratch_shapes=[dma(9)],
            compiler_params=pltpu.CompilerParams(vmem_limit_bytes=16 << 20),
            name="put_out",
        )(*(x for x in out))

    whole, cut_rows = P(None, None, None), P(None, "dp", None)
    return jax.shard_map(
        step,
        mesh=mesh,
        in_specs=(P(("rep", "dp"), None, None, None),) * 3 + (whole,) * 3 + (cut_rows,) * 6,
        out_specs=(P("rep", None, None),) * 3 + (P("rep", "dp", None),) * 6,
        check_vma=False,
    )
```

time: 232 us -> 230 us (level)
  Pallas kernels: 232 us -> 229 us
    pallas_call x1, Pallas kernels: 219 us -> 217 us  [step(): pl.pallas_call(functools.partial(kernel, size, count, pieces), out_shape=...]
where the time goes in v2:
time: 230 us
  Pallas kernels  229 us (100%)
    pallas_call x1, Pallas kernels, step(): pl.pallas_call(functools.partial(kernel, size, count, pieces), out_shape=...  217 us
    pallas_call x1, Pallas kernels, step(): pl.pallas_call(put_out, out_shape=[jax.ShapeDtypeStruct(x.shape, x.dtype)...  12.2 us

profile of v2, /device:TPU:113, one launch (start us, length us, event | category | flops | bytes accessed | tf_op | source)
XLA Modules:
  0.0 229.6 jit_solution(7417285583116032968)
XLA Ops:
  0.6 216.8 %step.1 = (bf16[2,896,2304]{2,1,0:T(8,128)(2,1)S(1)}, bf16[2,896,2304]{2,1,0:T(8,128)(2,1)S(1)}, bf16[2,2304,896]{2,1,0:T(8,128)(2,1)S(1)}, f32[2,112,2304]{2,1,...) custom-call(bf16[1,2,896,2304]{3,2,1,0:T(8,128)(2,1)} %refs_0_.1, ...), custom_call_target="tpu_custom_call" | custom-call | tf_op jit(solution)/shard_map/step/pallas_call | solution.py:283
  217.5 12.2 %put_out.1 = (bf16[2,896,2304]{2,1,0:T(8,128)(2,1)}, bf16[2,896,2304]{2,1,0:T(8,128)(2,1)}, bf16[2,2304,896]{2,1,0:T(8,128)(2,1)}, f32[2,112,2304]{2,1,0:T(8,128...) custom-call(bf16[2,896,2304]{2,1,0:T(8,128)(2,1)S(1)} %get-tuple-ele, ...), custom_call_target="tpu_custom_call" | custom-call | tf_op jit(solution)/shard_map/put_out/pallas_call | solution.py:307

commit v3 on v2

--- a/solution.py
+++ b/solution.py
@@ -32,24 +32,34 @@
     return pieces
 
 
+def seat(size):
+    chips = size // 2
+    me = lax.axis_index("dp")
+    chip, core = me // 2, lax.rem(me, 2)
+    at = lambda offset: lax.rem(chip + offset, chips)
+    return me, chip, core, at, chip * 2 + 1 - core, at(1) * 2 + core, at(chips - 1) * 2 + core
+
+
+def remote(source, target, send, recv, device):
+    return pltpu.make_async_remote_copy(source, target, send, recv, device_id={"dp": device}, device_id_type=MESH)
+
+
 def kernel(size, count, pieces, *refs):
     chips = size // 2
     take = iter(refs)
     some = lambda n: [next(take) for _ in range(n)]
     g_in, w_in, m_in, v_in = some(KINDS), some(KINDS), some(KINDS), some(KINDS)
-    W, M, V = some(KINDS), some(KINDS), some(KINDS)
+    W, M, V, (up, kept) = some(1), some(KINDS), some(KINDS), some(2)
+    W += some(KINDS - 1)
     old, hop, last = some(KINDS), some(KINDS), some(KINDS)
-    squares, own_sem, load_sem, peer_send, peer_recv, link_send, link_recv, sq_send, sq_recv = some(9)
-
-    me = lax.axis_index("dp")
-    chip, core = me // 2, lax.rem(me, 2)
-    at = lambda offset: lax.rem(chip + offset, chips)
-    sibling = chip * 2 + 1 - core
-    ahead, behind = at(1) * 2 + core, at(chips - 1) * 2 + core
+    squares, own_sem, load_sem, peer_send, peer_recv, link_send, link_recv, next_send, next_recv, sq_send, sq_recv = some(11)
+
+    me, chip, core, at, sibling, ahead, behind = seat(size)
     across = chips // 2
     offsets = (across, 1, chips - 1, 0)
     rows = [m.shape[1] for m in m_in]
     every = range(len(pieces))
+    ways = ((True, 0), (False, 1))
 
     barrier = pltpu.get_barrier_semaphore()
     for step in range(1, size):
@@ -84,14 +94,13 @@
     def give(o):
         for q in every:
             for l in range(LAYERS):
-                a = pieces[q][0]
-                given[o, l, q] = pltpu.make_async_remote_copy(
+                a, u = pieces[q][0], unit(o, l, q)
+                given[o, l, q] = remote(
                     g_in[a].at[0, l, block(q, theirs(o))],
                     W[a].at[l, block(q, mine(o))],
-                    peer_send.at[unit(o, l, q)],
-                    peer_recv.at[unit(o, l, q)],
-                    device_id={"dp": sibling},
-                    device_id_type=MESH,
+                    peer_send.at[u],
+                    peer_recv.at[u],
+                    sibling,
                 )
                 given[o, l, q].start()
 
@@ -127,13 +136,8 @@
 
     def to_link(forward, stage, q, source, target):
         slot = ((0 if forward else 1) * 3 + stage) * len(pieces) + q
-        sent[forward, stage, q] = pltpu.make_async_remote_copy(
-            source,
-            target,
-            link_send.at[slot],
-            link_recv.at[slot],
-            device_id={"dp": ahead if forward else behind},
-            device_id_type=MESH,
+        sent[forward, stage, q] = remote(
+            source, target, link_send.at[slot], link_recv.at[slot], ahead if forward else behind
         )
         sent[forward, stage, q].start()
 
@@ -144,7 +148,7 @@
         fetch(o)
         give(o)
     for q in every:
-        for forward, l in ((True, 0), (False, 1)):
+        for forward, l in ways:
             add(across, l, q)
             a = pieces[q][0]
             to_link(forward, 0, q, W[a].at[l, block(q, mine(across))], hop[a].at[l, part(q)])
@@ -166,7 +170,7 @@
                 loads.append(pltpu.make_async_copy(source, target, load_sem.at[(l * KINDS + a) * 3 + n]))
                 loads[-1].start()
     for q in every:
-        for forward, l in ((True, 0), (False, 1)):
+        for forward, l in ways:
             o = 1 if forward else chips - 1
             sent[forward, 0, q].wait_recv()
             a = pieces[q][0]
@@ -188,13 +192,8 @@
     told = []
     for step in range(1, size):
         told.append(
-            pltpu.make_async_remote_copy(
-                squares.at[me],
-                squares.at[me],
-                sq_send.at[step - 1],
-                sq_recv.at[step - 1],
-                device_id={"dp": lax.rem(me + step, size)},
-                device_id_type=MESH,
+            remote(
+                squares.at[me], squares.at[me], sq_send.at[step - 1], sq_recv.at[step - 1], lax.rem(me + step, size)
             )
         )
         told[-1].start()
@@ -207,15 +206,16 @@
         a = pieces[q][0]
 
         def body(start, height, carry):
+            its = pl.ds(start, height)
             here = W[a].at[l, block(q, me, start, height)]
-            its = pl.ds(start, height)
             g = here[...].astype(jnp.float32) * factor
             w = old[a][l, its].astype(jnp.float32)
             m = 0.9 * M[a][l, its] + 0.1 * g
             v = 0.95 * V[a][l, its] + 0.05 * g * g
             M[a][l, its] = m
             V[a][l, its] = v
-            here[...] = (w - 0.02 * (m * lax.rsqrt(v + 1e-8) + 0.1 * w)).astype(jnp.bfloat16)
+            to = here if a == 0 else up.at[l, chip, its] if a == 1 else kept.at[l, its]
+            to[...] = (w - 0.02 * (m * lax.rsqrt(v + 1e-8) + 0.1 * w)).astype(jnp.bfloat16)
             return carry
 
         each_strip(q, body, 0)
@@ -225,44 +225,228 @@
     def share(o, l, q):
         place = W[pieces[q][0]].at[l, block(q, mine(o))]
         u = unit(o, l, q)
-        shared.append(
-            pltpu.make_async_remote_copy(
-                place, place, peer_send.at[u], peer_recv.at[u], device_id={"dp": sibling}, device_id_type=MESH
-            )
-        )
+        shared.append(remote(place, place, peer_send.at[u], peer_recv.at[u], sibling))
         shared[-1].start()
 
     def pass_on(forward, stage, o, l, q):
         place = W[pieces[q][0]].at[l, block(q, mine(o))]
         to_link(forward, stage, q, place, place)
 
-    for q in every:
-        for forward, l in ((True, 0), (False, 1)):
+    now = [q for q in every if pieces[q][0] == 0]
+    for q in now:
+        for forward, l in ways:
             update(l, q)
             pass_on(forward, 0, 0, l, q)
-    for q in every:
+    for q in now:
         for forward, l in ((True, 1), (False, 0)):
             pass_on(forward, 1, 0, l, q)
             share(0, l, q)
+    for q in every:
+        if q not in now:
+            for l in range(LAYERS):
+                update(l, q)
+
+    later = {}
+    soon = [q for q in every if pieces[q][0] == 1]
     for stage in range(3):
-        for q in every:
-            for forward, l in ((True, 0), (False, 1)):
+        for i, q in enumerate(soon):
+            for forward, l in ways:
+                l = 1 - l if stage == 1 else l
+                o = 0 if stage < 2 else chips - 1 if forward else 1
+                slot = ((0 if forward else 1) * 3 + stage) * len(soon) + i
+                place = up.at[l, at(o), part(q)]
+                later[forward, stage, q] = remote(
+                    place, place, next_send.at[slot], next_recv.at[slot], ahead if forward else behind
+                )
+
+    for stage in range(3):
+        for q in now:
+            for forward, l in ways:
                 l = 1 - l if stage == 1 else l
                 sent[forward, stage, q].wait_recv()
                 o = across if stage == 2 else chips - 1 if forward else 1
                 if stage == 0:
                     pass_on(forward, 2, o, l, q)
                 share(o, l, q)
+        if stage == 0:
+
+            @pl.when(core == 1)
+            def _():
+                for (_, which, _), copy in later.items():
+                    if which < 2:
+                        copy.start()
+
     for copy in shared:
         copy.wait_recv()
-    for copy in (*shared, *sent.values(), *told):
+    for copy in (*shared, *told):
         copy.wait_send()
-
-
-def put_out(*refs):
+    for (_, _, q), copy in sent.items():
+        if q in now:
+            copy.wait_send()
+
+    @pl.when(core == 1)
+    def _():
+        for q in soon:
+            for forward, _ in ways:
+                later[forward, 0, q].wait_recv()
+                later[forward, 2, q].start()
+        for (_, which, _), copy in later.items():
+            if which > 0:
+                copy.wait_recv()
+        for copy in later.values():
+            copy.wait_send()
+
+
+def gather(size, pieces, after, up, kept, *refs):
+    W, (ready, peer_send, peer_recv, link_send, link_recv) = (None, *refs[:2]), refs[2:]
+    chips = size // 2
+    me, chip, core, at, sibling, ahead, behind = seat(size)
+    across = chips // 2
+    offsets = (across, 1, chips - 1, 0)
+    every = range(len(pieces))
+    ways = ((True, 0), (False, 1))
+    heights = (None, up.shape[2], kept.shape[1])
+
+    barrier = pltpu.get_barrier_semaphore()
+    for peer in (ahead, behind):
+        pl.semaphore_signal(barrier, inc=1, device_id={"dp": peer}, device_id_type=MESH)
+
+    @pl.when(core == 0)
+    def _():
+        pl.semaphore_signal(barrier, inc=1, device_id={"dp": sibling}, device_id_type=MESH)
+
+    pl.semaphore_wait(barrier, 2 + core)
+
+    @pl.when(core == 1)
+    def _():
+        pl.semaphore_signal(ready, inc=1, device_id={"dp": sibling}, device_id_type=MESH)
+
+    def target(o, l, q):
+        a, first, high = pieces[q]
+        return W[a].at[l, pl.ds(pl.multiple_of((at(o) * 2 + core) * heights[a] + first, 16), high)]
+
+    def held(o, l, q):
+        a, first, high = pieces[q]
+        return up.at[l, at(o), pl.ds(first, high)] if a == 1 else kept.at[l, pl.ds(first, high)]
+
+    sent, shares = {}, {}
+    for q in every:
+        for stage in range(3):
+            for forward, l in ways:
+                l = 1 - l if stage == 1 else l
+                o = 0 if stage < 2 else chips - 1 if forward else 1
+                slot = ((0 if forward else 1) * 3 + stage) * len(pieces) + q
+                sent[forward, stage, q] = remote(
+                    held(o, l, q) if o == 0 else target(o, l, q),
+                    target(o, l, q),
+                    link_send.at[slot],
+                    link_recv.at[slot],
+                    ahead if forward else behind,
+                )
+        for o in offsets:
+            for l in range(LAYERS):
+                u = (offsets.index(o) * LAYERS + l) * len(pieces) + q
+                for early in (False, True):
+                    source = held(o, l, q) if o == 0 or early else target(o, l, q)
+                    if not early or pieces[q][0] == 1:
+                        shares[o, l, q, early] = remote(source, target(o, l, q), peer_send.at[u], peer_recv.at[u], sibling)
+
+    first = [q for q in every if pieces[q][0] == 1]
+    then = [q for q in every if pieces[q][0] == 2]
+
+    @pl.when(core == 0)
+    def _():
+        for stage in range(2):
+            for q in first:
+                for forward, _ in ways:
+                    sent[forward, stage, q].start()
+
+    @pl.when(core == 1)
+    def _():
+        for stage in range(2):
+            for q in then:
+                for forward, _ in ways:
+                    sent[forward, stage, q].start()
+
+    def keep(o, a, blocks):
+        height = strip(blocks.shape[-1])
+        row = pl.multiple_of((at(o) * 2 + core) * heights[a], 16)
+
+        def body(i, carry):
+            start = pl.multiple_of(i * height, 16)
+            for l in range(LAYERS):
+                source = blocks.at[l, at(o), pl.ds(start, height)] if a == 1 else blocks.at[l, pl.ds(start, height)]
+                W[a][l, pl.ds(row + start, height)] = source[...]
+            return carry
+
+        lax.fori_loop(0, heights[a] // height, body, 0)
+
+    keep(0, 1, up)
+    keep(0, 2, kept)
+
+    @pl.when(core == 0)
+    def _():
+        for q in first:
+            for forward, _ in ways:
+                sent[forward, 0, q].wait_recv()
+                sent[forward, 2, q].start()
+        for stage in range(2):
+            for q in then:
+                for forward, _ in ways:
+                    sent[forward, stage, q].start()
+        for stage in (1, 2):
+            for q in first:
+                for forward, _ in ways:
+                    sent[forward, stage, q].wait_recv()
+        pl.semaphore_wait(ready, 1)
+        for o in offsets:
+            for l in range(LAYERS):
+                for q in first:
+                    shares[o, l, q, False].start()
+
+    @pl.when(core == 1)
+    def _():
+        for o in offsets:
+            for l in range(LAYERS):
+                for q in first:
+                    shares[o, l, q, True].start()
+        for o in offsets[:-1]:
+            keep(o, 1, up)
+
+    for l in range(LAYERS):
+        for q in then:
+            shares[0, l, q, False].start()
+    for stage in range(3):
+        for q in then:
+            for forward, l in ways:
+                l = 1 - l if stage == 1 else l
+                o = across if stage == 2 else chips - 1 if forward else 1
+                sent[forward, stage, q].wait_recv()
+                if stage == 0:
+                    sent[forward, 2, q].start()
+                shares[o, l, q, False].start()
+    for (_, _, _, early), copy in shares.items():
+        if not early:
+            copy.wait_recv()
+            copy.wait_send()
+    for (_, _, q), copy in sent.items():
+        if q in then:
+            copy.wait_send()
+
+    @pl.when(core == 0)
+    def _():
+        for (_, _, q), copy in sent.items():
+            if q in first:
+                copy.wait_send()
+
+
+def put_out(marked, *refs):
     *refs, sems = refs
-    n = len(refs) // 2
-    copies = [pltpu.make_async_copy(a, b, sems.at[i]) for i, (a, b) in enumerate(zip(refs[:n], refs[n:]))]
+    n = (len(refs) - marked) // 2
+    pairs = list(zip(refs[:n], refs[n:]))
+    if marked:
+        pairs.append((refs[1].at[0, pl.ds(0, 8), pl.ds(0, 128)], refs[-1]))
+    copies = [pltpu.make_async_copy(a, b, sems.at[i]) for i, (a, b) in enumerate(pairs)]
     for copy in copies:
         copy.start()
     for copy in copies:
@@ -275,20 +459,40 @@
     def step(*arrays):
         terms, weights, m, v = (arrays[i : i + 3] for i in (0, 3, 6, 9))
         count = size * sum(one.size for one in m)
-        in_vmem = [pltpu.VMEM(x.shape, x.dtype) for x in (*weights, *m, *v)]
-        blocks = [(LAYERS, *one.shape[1:]) for one in m]
+        vmem = lambda xs: [pltpu.VMEM(x.shape, x.dtype) for x in xs]
+        blocks = [pltpu.VMEM((LAYERS, *one.shape[1:]), jnp.bfloat16) for one in m]
+        pairs = [pltpu.VMEM((2, LAYERS, *one.shape[1:]), jnp.bfloat16) for one in m]
         dma = lambda n: pltpu.SemaphoreType.DMA((n,))
+        in_hbm, in_vmem = pl.BlockSpec(memory_space=pltpu.HBM), pl.BlockSpec(memory_space=pltpu.VMEM)
+        grant = 31 << 20
+
+        def put(marked, *results):
+            shapes = [jax.ShapeDtypeStruct(x.shape, x.dtype) for x in results]
+            shapes += [jax.ShapeDtypeStruct((8, 128), jnp.float32)] * marked
+            return pl.pallas_call(
+                functools.partial(put_out, marked),
+                out_shape=shapes,
+                in_specs=[in_vmem] * len(results),
+                out_specs=[in_hbm] * len(shapes),
+                scratch_shapes=[dma(len(shapes))],
+                compiler_params=pltpu.CompilerParams(vmem_limit_bytes=grant),
+                name="put_out",
+            )(*results)
+
         pieces = cut([one.shape[1] for one in m], [one.shape[2] for one in m])
         units, hops = 4 * LAYERS * len(pieces), 6 * len(pieces)
-        out = pl.pallas_call(
+        soon = sum(a == 1 for a, _, _ in pieces)
+        up_shape = pltpu.VMEM((LAYERS, size // 2, *m[1].shape[1:]), jnp.bfloat16)
+        *done, up, kept = pl.pallas_call(
             functools.partial(kernel, size, count, pieces),
-            out_shape=in_vmem,
-            in_specs=[pl.BlockSpec(memory_space=pltpu.HBM)] * 12,
-            out_specs=[pl.BlockSpec(memory_space=pltpu.VMEM)] * 9,
+            out_shape=[*vmem(weights[:1]), *vmem(m), *vmem(v), up_shape, blocks[-1]],
+            in_specs=[in_hbm] * 12,
+            out_specs=[in_vmem] * 9,
             scratch_shapes=[
-                *(pltpu.VMEM(b, jnp.bfloat16) for b in blocks),
-                *(pltpu.VMEM(b, jnp.bfloat16) for b in blocks),
-                *(pltpu.VMEM((2, *b), jnp.bfloat16) for b in blocks),
+                *vmem(weights[1:]),
+                *blocks,
+                *blocks,
+                *pairs,
                 pltpu.VMEM((size, 8, 128), jnp.float32),
                 dma(units),
                 dma(3 * LAYERS * KINDS),
@@ -296,23 +500,27 @@
                 dma(units),
                 dma(hops),
                 dma(hops),
+                dma(6 * soon),
+                dma(6 * soon),
                 dma(size - 1),
                 dma(size - 1),
             ],
-            compiler_params=pltpu.CompilerParams(
-                collective_id=0, has_side_effects=True, vmem_limit_bytes=16 << 20
-            ),
+            compiler_params=pltpu.CompilerParams(collective_id=0, has_side_effects=True, vmem_limit_bytes=grant),
             name="step",
         )(*(pltpu.with_memory_space_constraint(x, pltpu.HBM) for x in arrays))
-        return pl.pallas_call(
-            put_out,
-            out_shape=[jax.ShapeDtypeStruct(x.shape, x.dtype) for x in out],
-            in_specs=[pl.BlockSpec(memory_space=pltpu.VMEM)] * 9,
-            out_specs=[pl.BlockSpec(memory_space=pltpu.HBM)] * 9,
-            scratch_shapes=[dma(9)],
-            compiler_params=pltpu.CompilerParams(vmem_limit_bytes=16 << 20),
-            name="put_out",
-        )(*(x for x in out))
+        gate, *moments, after = put(1, *done)
+        ends = [piece for piece in pieces if piece[0] > 0]
+        units, hops = 4 * LAYERS * len(ends), 6 * len(ends)
+        rest = pl.pallas_call(
+            functools.partial(gather, size, ends),
+            out_shape=vmem(weights[1:]),
+            in_specs=[in_hbm, in_vmem, in_vmem],
+            out_specs=[in_vmem] * 2,
+            scratch_shapes=[pltpu.SemaphoreType.REGULAR, dma(units), dma(units), dma(hops), dma(hops)],
+            compiler_params=pltpu.CompilerParams(collective_id=1, has_side_effects=True, vmem_limit_bytes=grant),
+            name="gather",
+        )(after, up, kept)
+        return (gate, *put(0, *rest), *moments)
 
     whole, cut_rows = P(None, None, None), P(None, "dp", None)
     return jax.shard_map(

time: 230 us -> 223 us (0.970)
  Pallas kernels: 229 us -> 222 us
    pallas_call x1, Pallas kernels: 217 us -> 166 us  [step(): pl.pallas_call(functools.partial(kernel, size, count, pieces), out_shape=...]
    pallas_call x1 -> x3, Pallas kernels: 12.2 us -> 56.2 us  [the longest x1 42.9 us: step(): pl.pallas_call(functools.partial(gather, size, ends), out_shape=vmem(weig...]
where the time goes in v3:
time: 223 us
  Pallas kernels  222 us (100%)
    pallas_call x1, Pallas kernels, step(): pl.pallas_call(functools.partial(kernel, size, count, pieces), out_shape=...  166 us
    pallas_call x1, Pallas kernels, step(): pl.pallas_call(functools.partial(gather, size, ends), out_shape=vmem(weig...  42.9 us
    pallas_call x2, Pallas kernels, put(): pl.pallas_call(functools.partial(put_out, marked), out_shape=shapes, in_s...  13.3 us

profile of v3, /device:TPU:113, one launch (start us, length us, event | category | flops | bytes accessed | tf_op | source)
XLA Modules:
  0.0 222.8 jit_solution(9011840234900667340)
XLA Ops:
  0.6 165.9 %step.1 = (bf16[2,896,2304]{2,1,0:T(8,128)(2,1)S(1)}, f32[2,112,2304]{2,1,0:T(8,128)S(1)}, f32[2,112,2304]{2,1,0:T(8,128)S(1)}, f32[2,288,896]{2,1,0:T(8,128)S(1...) custom-call(bf16[1,2,896,2304]{3,2,1,0:T(8,128)(2,1)} %refs_0_.1, ...), custom_call_target="tpu_custom_call" | custom-call | tf_op jit(solution)/shard_map/step/pallas_call | solution.py:486
  166.6 7.2 %put_out.2 = (bf16[2,896,2304]{2,1,0:T(8,128)(2,1)}, f32[2,112,2304]{2,1,0:T(8,128)}, f32[2,112,2304]{2,1,0:T(8,128)}, f32[2,288,896]{2,1,0:T(8,128)}, f32[2,112...) custom-call(bf16[2,896,2304]{2,1,0:T(8,128)(2,1)S(1)} %get-tuple-element.30.refs_0_, ...), custom_call_target="tpu_custom_call" | custom-call | tf_op jit(solution)/shard_map/put_out/pallas_call | solution.py:472
  173.8 42.9 %gather.1 = (bf16[2,896,2304]{2,1,0:T(8,128)(2,1)S(1)}, bf16[2,2304,896]{2,1,0:T(8,128)(2,1)S(1)}) custom-call(f32[8,128]{1,0:T(8,128)S(1)} %get-tuple-element.38.after, bf16[2,4,112,2304]{3,2,1,0:T(8,128)(2,1)S(1)} %get-tuple-element.39.up, bf16[2,288,896]{2,1,0:T(8,128)(2,1)S(1)} %get-tuple-element.40.kept), custom_call_target="tpu_custom_call" | custom-call | tf_op jit(solution)/shard_map/gather/pallas_call | solution.py:514
  216.7 6.1 %put_out.3 = (bf16[2,896,2304]{2,1,0:T(8,128)(2,1)}, bf16[2,2304,896]{2,1,0:T(8,128)(2,1)}) custom-call(bf16[2,896,2304]{2,1,0:T(8,128)(2,1)S(1)} %get-tuple-element.41.refs_0_, bf16[2,2304,896]{2,1,0:T(8,128)(2,1)S(1)} %get-tuple-element.42.refs_1_), custom_call_target="tpu_custom_call" | custom-call | tf_op jit(solution)/shard_map/put_out/pallas_call | solution.py:472

commit v4 on v3

--- a/solution.py
+++ b/solution.py
@@ -9,6 +9,7 @@
 
 LAYERS = 2
 KINDS = 3
+STAGES = 3
 MESH = pl.DeviceIdType.MESH
 
 
@@ -49,7 +50,7 @@
     take = iter(refs)
     some = lambda n: [next(take) for _ in range(n)]
     g_in, w_in, m_in, v_in = some(KINDS), some(KINDS), some(KINDS), some(KINDS)
-    W, M, V, (up, kept) = some(1), some(KINDS), some(KINDS), some(2)
+    W, M, V, kept, (early,) = some(1), some(KINDS), some(KINDS), some(KINDS - 1), some(1)
     W += some(KINDS - 1)
     old, hop, last = some(KINDS), some(KINDS), some(KINDS)
     squares, own_sem, load_sem, peer_send, peer_recv, link_send, link_recv, next_send, next_recv, sq_send, sq_recv = some(11)
@@ -214,7 +215,7 @@
             v = 0.95 * V[a][l, its] + 0.05 * g * g
             M[a][l, its] = m
             V[a][l, its] = v
-            to = here if a == 0 else up.at[l, chip, its] if a == 1 else kept.at[l, its]
+            to = here if a == 0 else kept[a - 1].at[l, its]
             to[...] = (w - 0.02 * (m * lax.rsqrt(v + 1e-8) + 0.1 * w)).astype(jnp.bfloat16)
             return carry
 
@@ -254,9 +255,13 @@
                 l = 1 - l if stage == 1 else l
                 o = 0 if stage < 2 else chips - 1 if forward else 1
                 slot = ((0 if forward else 1) * 3 + stage) * len(soon) + i
-                place = up.at[l, at(o), part(q)]
+                place = early.at[l, at(o), part(q)]
                 later[forward, stage, q] = remote(
-                    place, place, next_send.at[slot], next_recv.at[slot], ahead if forward else behind
+                    kept[0].at[l, part(q)] if o == 0 else place,
+                    place,
+                    next_send.at[slot],
+                    next_recv.at[slot],
+                    ahead if forward else behind,
                 )
 
     for stage in range(3):
@@ -297,15 +302,23 @@
             copy.wait_send()
 
 
-def gather(size, pieces, after, up, kept, *refs):
-    W, (ready, peer_send, peer_recv, link_send, link_recv) = (None, *refs[:2]), refs[2:]
+def gather(size, pieces, done, more, ahead_of, after, *refs):
+    take = iter(refs)
+    some = lambda n: [next(take) for _ in range(n)]
+    kept, early = some(2)
+    (kept_next,) = some(1) if more else (None,)
+    (W,) = some(1)
+    (early_next,) = some(1) if more else (None,)
+    ready, peer_send, peer_recv, link_send, link_recv = some(5)
+    next_send, next_recv = some(2) if more else (None, None)
+
     chips = size // 2
     me, chip, core, at, sibling, ahead, behind = seat(size)
     across = chips // 2
     offsets = (across, 1, chips - 1, 0)
-    every = range(len(pieces))
     ways = ((True, 0), (False, 1))
-    heights = (None, up.shape[2], kept.shape[1])
+    rows = kept.shape[1]
+    height = strip(kept.shape[-1])
 
     barrier = pltpu.get_barrier_semaphore()
     for peer in (ahead, behind):
@@ -321,123 +334,122 @@
     def _():
         pl.semaphore_signal(ready, inc=1, device_id={"dp": sibling}, device_id_type=MESH)
 
-    def target(o, l, q):
-        a, first, high = pieces[q]
-        return W[a].at[l, pl.ds(pl.multiple_of((at(o) * 2 + core) * heights[a] + first, 16), high)]
-
-    def held(o, l, q):
-        a, first, high = pieces[q]
-        return up.at[l, at(o), pl.ds(first, high)] if a == 1 else kept.at[l, pl.ds(first, high)]
-
-    sent, shares = {}, {}
-    for q in every:
+    def row(o, start):
+        return pl.multiple_of((at(o) * 2 + core) * rows + start, 16)
+
+    def hop(forward, stage):
+        l = 0 if forward == (stage != 1) else 1
+        behind_it = chips - 1 if forward else 1
+        return l, 0 if stage < 2 else behind_it, behind_it if stage < 2 else across
+
+    sent, rest, later, shares = {}, {}, {}, {}
+    for i, (first, high) in enumerate(pieces):
         for stage in range(3):
-            for forward, l in ways:
-                l = 1 - l if stage == 1 else l
-                o = 0 if stage < 2 else chips - 1 if forward else 1
-                slot = ((0 if forward else 1) * 3 + stage) * len(pieces) + q
-                sent[forward, stage, q] = remote(
-                    held(o, l, q) if o == 0 else target(o, l, q),
-                    target(o, l, q),
-                    link_send.at[slot],
-                    link_recv.at[slot],
+            for forward, _ in ways:
+                l, o, _ = hop(forward, stage)
+                slot = ((0 if forward else 1) * 3 + stage) * len(pieces) + i
+                target = W.at[l, pl.ds(row(o, first), high)]
+                its = link_send.at[slot], link_recv.at[slot], ahead if forward else behind
+                sent[forward, stage, i] = remote(kept.at[l, pl.ds(first, high)] if o == 0 else target, target, *its)
+                if stage >= done:
+                    rest[forward, stage, i] = remote(early.at[l, at(o), pl.ds(first, high)], target, *its)
+        for o in offsets:
+            for l in range(LAYERS):
+                u = (offsets.index(o) * LAYERS + l) * len(pieces) + i
+                target = W.at[l, pl.ds(row(o, first), high)]
+                held = early.at[l, at(o), pl.ds(first, high)]
+                for one in range(2):
+                    source = kept.at[l, pl.ds(first, high)] if o == 0 else held if one and (o != across or done == 3) else target
+                    shares[one, o, l, i] = remote(source, target, peer_send.at[u], peer_recv.at[u], sibling)
+    for i, (first, high) in enumerate(more):
+        for stage in range(ahead_of):
+            for forward, _ in ways:
+                l, o, _ = hop(forward, stage)
+                slot = ((0 if forward else 1) * 3 + stage) * len(more) + i
+                target = early_next.at[l, at(o), pl.ds(first, high)]
+                later[forward, stage, i] = remote(
+                    kept_next.at[l, pl.ds(first, high)] if o == 0 else target,
+                    target,
+                    next_send.at[slot],
+                    next_recv.at[slot],
                     ahead if forward else behind,
                 )
-        for o in offsets:
+
+    def keep(o):
+        def body(n, carry):
+            start = pl.multiple_of(n * height, 16)
             for l in range(LAYERS):
-                u = (offsets.index(o) * LAYERS + l) * len(pieces) + q
-                for early in (False, True):
-                    source = held(o, l, q) if o == 0 or early else target(o, l, q)
-                    if not early or pieces[q][0] == 1:
-                        shares[o, l, q, early] = remote(source, target(o, l, q), peer_send.at[u], peer_recv.at[u], sibling)
-
-    first = [q for q in every if pieces[q][0] == 1]
-    then = [q for q in every if pieces[q][0] == 2]
+                source = kept.at[l, pl.ds(start, height)] if o == 0 else early.at[l, at(o), pl.ds(start, height)]
+                W[l, pl.ds(row(o, start), height)] = source[...]
+            return carry
+
+        lax.fori_loop(0, rows // height, body, 0)
+
+    each = range(len(pieces))
 
     @pl.when(core == 0)
     def _():
         for stage in range(2):
-            for q in first:
+            for i in each:
                 for forward, _ in ways:
-                    sent[forward, stage, q].start()
+                    sent[forward, stage, i].start()
+        keep(0)
+        for i in each:
+            for forward, _ in ways:
+                sent[forward, 0, i].wait_recv()
+                sent[forward, 2, i].start()
+        pl.semaphore_wait(ready, 1)
+        for i in each:
+            for l in range(LAYERS):
+                shares[0, 0, l, i].start()
+        for stage in range(3):
+            for i in each:
+                for forward, _ in ways:
+                    l, _, o = hop(forward, stage)
+                    if stage > 0:
+                        sent[forward, stage, i].wait_recv()
+                    shares[0, o, l, i].start()
+        for copy in sent.values():
+            copy.wait_send()
 
     @pl.when(core == 1)
     def _():
-        for stage in range(2):
-            for q in then:
-                for forward, _ in ways:
-                    sent[forward, stage, q].start()
-
-    def keep(o, a, blocks):
-        height = strip(blocks.shape[-1])
-        row = pl.multiple_of((at(o) * 2 + core) * heights[a], 16)
-
-        def body(i, carry):
-            start = pl.multiple_of(i * height, 16)
-            for l in range(LAYERS):
-                source = blocks.at[l, at(o), pl.ds(start, height)] if a == 1 else blocks.at[l, pl.ds(start, height)]
-                W[a][l, pl.ds(row + start, height)] = source[...]
-            return carry
-
-        lax.fori_loop(0, heights[a] // height, body, 0)
-
-    keep(0, 1, up)
-    keep(0, 2, kept)
-
-    @pl.when(core == 0)
-    def _():
-        for q in first:
+        for copy in rest.values():
+            copy.start()
+        for (_, stage, _), copy in later.items():
+            if stage < 2:
+                copy.start()
+        here = [o for o in offsets if o != across or done == 3]
+        for o in here:
+            for i in each:
+                for l in range(LAYERS):
+                    shares[1, o, l, i].start()
+        for o in here:
+            keep(o)
+        for (forward, stage, i), copy in rest.items():
+            l, _, o = hop(forward, stage)
+            copy.wait_recv()
+            shares[1, o, l, i].start()
+        for i in range(len(more)):
             for forward, _ in ways:
-                sent[forward, 0, q].wait_recv()
-                sent[forward, 2, q].start()
-        for stage in range(2):
-            for q in then:
-                for forward, _ in ways:
-                    sent[forward, stage, q].start()
-        for stage in (1, 2):
-            for q in first:
-                for forward, _ in ways:
-                    sent[forward, stage, q].wait_recv()
-        pl.semaphore_wait(ready, 1)
-        for o in offsets:
-            for l in range(LAYERS):
-                for q in first:
-                    shares[o, l, q, False].start()
+                later[forward, 0, i].wait_recv()
+                if ahead_of == 3:
+                    later[forward, 2, i].start()
+
+    for (one, _, _, _), copy in shares.items():
+        if one == 0:
+            copy.wait_recv()
+            copy.wait_send()
 
     @pl.when(core == 1)
     def _():
-        for o in offsets:
-            for l in range(LAYERS):
-                for q in first:
-                    shares[o, l, q, True].start()
-        for o in offsets[:-1]:
-            keep(o, 1, up)
-
-    for l in range(LAYERS):
-        for q in then:
-            shares[0, l, q, False].start()
-    for stage in range(3):
-        for q in then:
-            for forward, l in ways:
-                l = 1 - l if stage == 1 else l
-                o = across if stage == 2 else chips - 1 if forward else 1
-                sent[forward, stage, q].wait_recv()
-                if stage == 0:
-                    sent[forward, 2, q].start()
-                shares[o, l, q, False].start()
-    for (_, _, _, early), copy in shares.items():
-        if not early:
-            copy.wait_recv()
+        for copy in rest.values():
             copy.wait_send()
-    for (_, _, q), copy in sent.items():
-        if q in then:
+        for (_, stage, _), copy in later.items():
+            if stage > 0:
+                copy.wait_recv()
+        for copy in later.values():
             copy.wait_send()
-
-    @pl.when(core == 0)
-    def _():
-        for (_, _, q), copy in sent.items():
-            if q in first:
-                copy.wait_send()
 
 
 def put_out(marked, *refs):
@@ -445,7 +457,7 @@
     n = (len(refs) - marked) // 2
     pairs = list(zip(refs[:n], refs[n:]))
     if marked:
-        pairs.append((refs[1].at[0, pl.ds(0, 8), pl.ds(0, 128)], refs[-1]))
+        pairs.append((refs[0].at[0, pl.ds(0, 16), pl.ds(0, 128)], refs[-1]))
     copies = [pltpu.make_async_copy(a, b, sems.at[i]) for i, (a, b) in enumerate(pairs)]
     for copy in copies:
         copy.start()
@@ -468,7 +480,7 @@
 
         def put(marked, *results):
             shapes = [jax.ShapeDtypeStruct(x.shape, x.dtype) for x in results]
-            shapes += [jax.ShapeDtypeStruct((8, 128), jnp.float32)] * marked
+            shapes += [jax.ShapeDtypeStruct((16, 128), jnp.bfloat16)] * marked
             return pl.pallas_call(
                 functools.partial(put_out, marked),
                 out_shape=shapes,
@@ -482,12 +494,12 @@
         pieces = cut([one.shape[1] for one in m], [one.shape[2] for one in m])
         units, hops = 4 * LAYERS * len(pieces), 6 * len(pieces)
         soon = sum(a == 1 for a, _, _ in pieces)
-        up_shape = pltpu.VMEM((LAYERS, size // 2, *m[1].shape[1:]), jnp.bfloat16)
-        *done, up, kept = pl.pallas_call(
+        early = [pltpu.VMEM((LAYERS, size // 2, *one.shape[1:]), jnp.bfloat16) for one in m]
+        *done, kept_up, kept_down, early_up = pl.pallas_call(
             functools.partial(kernel, size, count, pieces),
-            out_shape=[*vmem(weights[:1]), *vmem(m), *vmem(v), up_shape, blocks[-1]],
+            out_shape=[*vmem(weights[:1]), *vmem(m), *vmem(v), *blocks[1:], early[1]],
             in_specs=[in_hbm] * 12,
-            out_specs=[in_vmem] * 9,
+            out_specs=[in_vmem] * 10,
             scratch_shapes=[
                 *vmem(weights[1:]),
                 *blocks,
@@ -509,18 +521,33 @@
             name="step",
         )(*(pltpu.with_memory_space_constraint(x, pltpu.HBM) for x in arrays))
         gate, *moments, after = put(1, *done)
-        ends = [piece for piece in pieces if piece[0] > 0]
-        units, hops = 4 * LAYERS * len(ends), 6 * len(ends)
-        rest = pl.pallas_call(
-            functools.partial(gather, size, ends),
-            out_shape=vmem(weights[1:]),
-            in_specs=[in_hbm, in_vmem, in_vmem],
-            out_specs=[in_vmem] * 2,
-            scratch_shapes=[pltpu.SemaphoreType.REGULAR, dma(units), dma(units), dma(hops), dma(hops)],
-            compiler_params=pltpu.CompilerParams(collective_id=1, has_side_effects=True, vmem_limit_bytes=grant),
-            name="gather",
-        )(after, up, kept)
-        return (gate, *put(0, *rest), *moments)
+        ends = [[(first, high) for kind, first, high in pieces if kind == a] for a in range(KINDS)]
+
+        def finish(a, done, ahead_of, *held):
+            more = ends[a + 1] if ahead_of else []
+            units, hops = 4 * LAYERS * len(ends[a]), 6 * len(ends[a])
+            return pl.pallas_call(
+                functools.partial(gather, size, ends[a], done, more, ahead_of),
+                out_shape=[*vmem(weights[a : a + 1]), *(early[a + 1 : a + 2] if more else [])],
+                in_specs=[in_hbm] + [in_vmem] * (len(held) - 1),
+                out_specs=[in_vmem] * (2 if more else 1),
+                scratch_shapes=[
+                    pltpu.SemaphoreType.REGULAR,
+                    dma(units),
+                    dma(units),
+                    dma(hops),
+                    dma(hops),
+                    *([dma(6 * len(more))] * 2 if more else []),
+                ],
+                compiler_params=pltpu.CompilerParams(collective_id=a, has_side_effects=True, vmem_limit_bytes=grant),
+                name=f"gather_{a}",
+            )(*held)
+
+        up, early_down = finish(1, 3, STAGES, after, kept_up, early_up, kept_down)
+        up, after = put(1, up)
+        (down,) = finish(2, STAGES, 0, after, kept_down, early_down)
+        (down,) = put(0, down)
+        return (gate, up, down, *moments)
 
     whole, cut_rows = P(None, None, None), P(None, "dp", None)
     return jax.shard_map(

time: 223 us -> 220 us (0.987)
  Pallas kernels: 222 us -> 219 us
    pallas_call x1 -> x2, Pallas kernels: 42.9 us -> 39.2 us  [finish(): pl.pallas_call(functools.partial(gather, size, ends[a], done, more, ahead...]
    pallas_call x2 -> x3, Pallas kernels: 13.3 us -> 13.9 us  [put(): pl.pallas_call(functools.partial(put_out, marked), out_shape=shapes, in_s...]
where the time goes in v4:
time: 220 us
  Pallas kernels  219 us (100%)
    pallas_call x1, Pallas kernels, step(): pl.pallas_call(functools.partial(kernel, size, count, pieces), out_shape=...  166 us
    pallas_call x2, Pallas kernels, finish(): pl.pallas_call(functools.partial(gather, size, ends[a], done, more, ahead...  39.2 us
    pallas_call x3, Pallas kernels, put(): pl.pallas_call(functools.partial(put_out, marked), out_shape=shapes, in_s...  13.9 us

profile of v4, /device:TPU:113, one launch (start us, length us, event | category | flops | bytes accessed | tf_op | source)
XLA Modules:
  0.0 219.8 jit_solution(5985331949362061256)
XLA Ops:
  0.6 165.9 %step.1 = (bf16[2,896,2304]{2,1,0:T(8,128)(2,1)S(1)}, f32[2,112,2304]{2,1,0:T(8,128)S(1)}, f32[2,112,2304]{2,1,0:T(8,128)S(1)}, f32[2,288,896]{2,1,0:T(8,128)S(1...) custom-call(bf16[1,2,896,2304]{3,2,1,0:T(8,128)(2,1)} %refs_0_.1, ...), custom_call_target="tpu_custom_call" | custom-call | tf_op jit(solution)/shard_map/step/pallas_call | solution.py:498
  166.6 7.2 %put_out.3 = (bf16[2,896,2304]{2,1,0:T(8,128)(2,1)}, f32[2,112,2304]{2,1,0:T(8,128)}, f32[2,112,2304]{2,1,0:T(8,128)}, f32[2,288,896]{2,1,0:T(8,128)}, f32[2,112...) custom-call(bf16[2,896,2304]{2,1,0:T(8,128)(2,1)S(1)} %get-tuple-element.31.refs, ...), custom_call_target="tpu_custom_call" | custom-call | tf_op jit(solution)/shard_map/put_out/pallas_call | solution.py:484
  173.8 26.7 %gather_1.1 = (bf16[2,896,2304]{2,1,0:T(8,128)(2,1)S(1)}, bf16[2,4,288,896]{3,2,1,0:T(8,128)(2,1)S(1)}) custom-call(bf16[16,128]{1,0:T(8,128)(2,1)S(1)} %get-tuple-element.39.after, bf16[2,112,2304]{2,1,0:T(8,128)(2,1)S(1)} %get-tuple-element.40.refs_0_, bf16[2,4,112,2304]{3,2,1,0:T(8,128)(2,1)S(1)} %get-tuple-element.41.refs_1_, ...), custom_call_target="tpu_custom_call" | custom-call | tf_op jit(solution)/shard_map/gather_1/pallas_call | solution.py:529
  200.5 3.4 %put_out.4 = (bf16[2,896,2304]{2,1,0:T(8,128)(2,1)}, bf16[16,128]{1,0:T(8,128)(2,1)S(1)}) custom-call(bf16[2,896,2304]{2,1,0:T(8,128)(2,1)S(1)} %get-tuple-element.43.refs_0_), custom_call_target="tpu_custom_call" | custom-call | tf_op jit(solution)/shard_map/put_out/pallas_call | solution.py:484
  203.8 12.6 %gather_2.1.refs_0_ = bf16[2,2304,896]{2,1,0:T(8,128)(2,1)S(1)} custom-call(bf16[16,128]{1,0:T(8,128)(2,1)S(1)} %get-tuple-element.45.after, bf16[2,288,896]{2,1,0:T(8,128)(2,1)S(1)} %get-tuple-element.42.refs_2_.refs_0_, bf16[2,4,288,896]{3,2,1,0:T(8,128)(2,1)S(1)} %get-tuple-element.46.refs_1_), custom_call_target="tpu_custom_call" | custom-call | tf_op jit(solution)/shard_map/gather_2/pallas_call | solution.py:529
  216.4 3.4 %put_out.5 = bf16[2,2304,896]{2,1,0:T(8,128)(2,1)} custom-call(bf16[2,2304,896]{2,1,0:T(8,128)(2,1)S(1)} %gather_2.1.refs_0_), custom_call_target="tpu_custom_call" | custom-call | tf_op jit(solution)/shard_map/put_out/pallas_call | solution.py:484

commit v5 on v4

--- a/solution.py
+++ b/solution.py
@@ -53,7 +53,7 @@
     W, M, V, kept, (early,) = some(1), some(KINDS), some(KINDS), some(KINDS - 1), some(1)
     W += some(KINDS - 1)
     old, hop, last = some(KINDS), some(KINDS), some(KINDS)
-    squares, own_sem, load_sem, peer_send, peer_recv, link_send, link_recv, next_send, next_recv, sq_send, sq_recv = some(11)
+    squares, own_sem, load_sem, peer_send, peer_recv, link_send, link_recv, next_send, next_recv, sq_send, sq_recv, met = some(12)
 
     me, chip, core, at, sibling, ahead, behind = seat(size)
     across = chips // 2
@@ -63,8 +63,6 @@
     ways = ((True, 0), (False, 1))
 
     barrier = pltpu.get_barrier_semaphore()
-    for step in range(1, size):
-        pl.semaphore_signal(barrier, inc=1, device_id={"dp": lax.rem(me + step, size)}, device_id_type=MESH)
 
     def block(q, device, start=None, height=None):
         a, first, high = pieces[q]
@@ -142,17 +140,47 @@
         )
         sent[forward, stage, q].start()
 
+    @pl.when(core == 1)
+    def _():
+        pl.semaphore_signal(barrier, inc=1, device_id={"dp": sibling}, device_id_type=MESH)
+
     fetch(across)
-    pl.semaphore_wait(barrier, size - 1)
+
+    @pl.when(core == 0)
+    def _():
+        pl.semaphore_wait(barrier, 1)
+        pl.semaphore_signal(met, inc=1, device_id={"dp": sibling}, device_id_type=MESH)
+
+    @pl.when(core == 1)
+    def _():
+        pl.semaphore_wait(met, 1)
+        for peer in (ahead, behind):
+            pl.semaphore_signal(barrier, inc=1, device_id={"dp": peer}, device_id_type=MESH)
+
     give(across)
-    for o in (1, chips - 1):
-        fetch(o)
-        give(o)
+
+    def greeted():
+        @pl.when(core == 1)
+        def _():
+            pl.semaphore_wait(barrier, 2)
+            pl.semaphore_signal(met, inc=1, device_id={"dp": sibling}, device_id_type=MESH)
+
+        @pl.when(core == 0)
+        def _():
+            pl.semaphore_wait(met, 1)
+
     for q in every:
+        for _, l in ways:
+            add(across, l, q)
+        if q == 0:
+            greeted()
         for forward, l in ways:
-            add(across, l, q)
             a = pieces[q][0]
             to_link(forward, 0, q, W[a].at[l, block(q, mine(across))], hop[a].at[l, part(q)])
+        if q == 0:
+            for o in (1, chips - 1):
+                fetch(o)
+                give(o)
     fetch(0)
     give(0)
     for q in every:
@@ -516,6 +544,7 @@
                 dma(6 * soon),
                 dma(size - 1),
                 dma(size - 1),
+                pltpu.SemaphoreType.REGULAR,
             ],
             compiler_params=pltpu.CompilerParams(collective_id=0, has_side_effects=True, vmem_limit_bytes=grant),
             name="step",

time: 220 us -> 219 us (level)
  no operation moved by 1% of the time
where the time goes in v5:
time: 219 us
  Pallas kernels  218 us (100%)
    pallas_call x1, Pallas kernels, step(): pl.pallas_call(functools.partial(kernel, size, count, pieces), out_shape=...  164 us
    pallas_call x2, Pallas kernels, finish(): pl.pallas_call(functools.partial(gather, size, ends[a], done, more, ahead...  39.5 us
    pallas_call x3, Pallas kernels, put(): pl.pallas_call(functools.partial(put_out, marked), out_shape=shapes, in_s...  13.9 us

profile of v5, /device:TPU:113, one launch (start us, length us, event | category | flops | bytes accessed | tf_op | source)
XLA Modules:
  0.0 218.5 jit_solution(5518511327509399207)
XLA Ops:
  0.6 164.4 %step.1 = (bf16[2,896,2304]{2,1,0:T(8,128)(2,1)S(1)}, f32[2,112,2304]{2,1,0:T(8,128)S(1)}, f32[2,112,2304]{2,1,0:T(8,128)S(1)}, f32[2,288,896]{2,1,0:T(8,128)S(1...) custom-call(bf16[1,2,896,2304]{3,2,1,0:T(8,128)(2,1)} %refs_0_.1, ...), custom_call_target="tpu_custom_call" | custom-call | tf_op jit(solution)/shard_map/step/pallas_call | solution.py:526
  165.1 7.2 %put_out.3 = (bf16[2,896,2304]{2,1,0:T(8,128)(2,1)}, f32[2,112,2304]{2,1,0:T(8,128)}, f32[2,112,2304]{2,1,0:T(8,128)}, f32[2,288,896]{2,1,0:T(8,128)}, f32[2,112...) custom-call(bf16[2,896,2304]{2,1,0:T(8,128)(2,1)S(1)} %get-tuple-element.31.refs, ...), custom_call_target="tpu_custom_call" | custom-call | tf_op jit(solution)/shard_map/put_out/pallas_call | solution.py:512
  172.3 26.7 %gather_1.1 = (bf16[2,896,2304]{2,1,0:T(8,128)(2,1)S(1)}, bf16[2,4,288,896]{3,2,1,0:T(8,128)(2,1)S(1)}) custom-call(bf16[16,128]{1,0:T(8,128)(2,1)S(1)} %get-tuple-element.39.after, bf16[2,112,2304]{2,1,0:T(8,128)(2,1)S(1)} %get-tuple-element.40.refs_0_, bf16[2,4,112,2304]{3,2,1,0:T(8,128)(2,1)S(1)} %get-tuple-element.41.refs_1_, ...), custom_call_target="tpu_custom_call" | custom-call | tf_op jit(solution)/shard_map/gather_1/pallas_call | solution.py:558
  199.0 3.4 %put_out.4 = (bf16[2,896,2304]{2,1,0:T(8,128)(2,1)}, bf16[16,128]{1,0:T(8,128)(2,1)S(1)}) custom-call(bf16[2,896,2304]{2,1,0:T(8,128)(2,1)S(1)} %get-tuple-element.43.refs_0_), custom_call_target="tpu_custom_call" | custom-call | tf_op jit(solution)/shard_map/put_out/pallas_call | solution.py:512
  202.4 12.8 %gather_2.1.refs_0_ = bf16[2,2304,896]{2,1,0:T(8,128)(2,1)S(1)} custom-call(bf16[16,128]{1,0:T(8,128)(2,1)S(1)} %get-tuple-element.45.after, bf16[2,288,896]{2,1,0:T(8,128)(2,1)S(1)} %get-tuple-element.42.refs_2_.refs_0_, bf16[2,4,288,896]{3,2,1,0:T(8,128)(2,1)S(1)} %get-tuple-element.46.refs_1_), custom_call_target="tpu_custom_call" | custom-call | tf_op jit(solution)/shard_map/gather_2/pallas_call | solution.py:558
  215.2 3.4 %put_out.5 = bf16[2,2304,896]{2,1,0:T(8,128)(2,1)} custom-call(bf16[2,2304,896]{2,1,0:T(8,128)(2,1)S(1)} %gather_2.1.refs_0_), custom_call_target="tpu_custom_call" | custom-call | tf_op jit(solution)/shard_map/put_out/pallas_call | solution.py:512

commit v6 on v5

--- a/solution.py
+++ b/solution.py
@@ -28,7 +28,7 @@
     pieces = []
     for a in range(KINDS):
         small = strip(columns[a])
-        heights = [small, rows[a] - small] if a == 0 else [rows[a]] if a < KINDS - 1 else [rows[a] - small, small]
+        heights = [small, 3 * small, rows[a] - 5 * small, small] if a == 0 else [rows[a]] if a < KINDS - 1 else [rows[a] - small, small]
         pieces += [(a, sum(heights[:i]), h) for i, h in enumerate(heights)]
     return pieces
 

time: 219 us -> 219 us (level)
  no operation moved by 1% of the time
where the time goes in v6:
time: 219 us; the launch traced here: 218 us
  Pallas kernels  218 us (100%)
    pallas_call x1, Pallas kernels, step(): pl.pallas_call(functools.partial(kernel, size, count, pieces), out_shape=...  166 us
    pallas_call x2, Pallas kernels, finish(): pl.pallas_call(functools.partial(gather, size, ends[a], done, more, ahead...  38.3 us
    pallas_call x3, Pallas kernels, put(): pl.pallas_call(functools.partial(put_out, marked), out_shape=shapes, in_s...  13.9 us

profile of v6, /device:TPU:113, one launch (start us, length us, event | category | flops | bytes accessed | tf_op | source)
XLA Modules:
  0.0 218.5 jit_solution(1468190122294518103)
XLA Ops:
  0.6 165.5 %step.1 = (bf16[2,896,2304]{2,1,0:T(8,128)(2,1)S(1)}, f32[2,112,2304]{2,1,0:T(8,128)S(1)}, f32[2,112,2304]{2,1,0:T(8,128)S(1)}, f32[2,288,896]{2,1,0:T(8,128)S(1...) custom-call(bf16[1,2,896,2304]{3,2,1,0:T(8,128)(2,1)} %refs_0_.1, ...), custom_call_target="tpu_custom_call" | custom-call | tf_op jit(solution)/shard_map/step/pallas_call | solution.py:526
  166.2 7.2 %put_out.3 = (bf16[2,896,2304]{2,1,0:T(8,128)(2,1)}, f32[2,112,2304]{2,1,0:T(8,128)}, f32[2,112,2304]{2,1,0:T(8,128)}, f32[2,288,896]{2,1,0:T(8,128)}, f32[2,112...) custom-call(bf16[2,896,2304]{2,1,0:T(8,128)(2,1)S(1)} %get-tuple-element.31.refs, ...), custom_call_target="tpu_custom_call" | custom-call | tf_op jit(solution)/shard_map/put_out/pallas_call | solution.py:512
  173.4 26.7 %gather_1.1 = (bf16[2,896,2304]{2,1,0:T(8,128)(2,1)S(1)}, bf16[2,4,288,896]{3,2,1,0:T(8,128)(2,1)S(1)}) custom-call(bf16[16,128]{1,0:T(8,128)(2,1)S(1)} %get-tuple-element.39.after, bf16[2,112,2304]{2,1,0:T(8,128)(2,1)S(1)} %get-tuple-element.40.refs_0_, bf16[2,4,112,2304]{3,2,1,0:T(8,128)(2,1)S(1)} %get-tuple-element.41.refs_1_, ...), custom_call_target="tpu_custom_call" | custom-call | tf_op jit(solution)/shard_map/gather_1/pallas_call | solution.py:558
  200.1 3.4 %put_out.4 = (bf16[2,896,2304]{2,1,0:T(8,128)(2,1)}, bf16[16,128]{1,0:T(8,128)(2,1)S(1)}) custom-call(bf16[2,896,2304]{2,1,0:T(8,128)(2,1)S(1)} %get-tuple-element.43.refs_0_), custom_call_target="tpu_custom_call" | custom-call | tf_op jit(solution)/shard_map/put_out/pallas_call | solution.py:512
  203.5 11.6 %gather_2.1.refs_0_ = bf16[2,2304,896]{2,1,0:T(8,128)(2,1)S(1)} custom-call(bf16[16,128]{1,0:T(8,128)(2,1)S(1)} %get-tuple-element.45.after, bf16[2,288,896]{2,1,0:T(8,128)(2,1)S(1)} %get-tuple-element.42.refs_2_.refs_0_, bf16[2,4,288,896]{3,2,1,0:T(8,128)(2,1)S(1)} %get-tuple-element.46.refs_1_), custom_call_target="tpu_custom_call" | custom-call | tf_op jit(solution)/shard_map/gather_2/pallas_call | solution.py:558
  215.1 3.4 %put_out.5 = bf16[2,2304,896]{2,1,0:T(8,128)(2,1)} custom-call(bf16[2,2304,896]{2,1,0:T(8,128)(2,1)S(1)} %gather_2.1.refs_0_), custom_call_target="tpu_custom_call" | custom-call | tf_op jit(solution)/shard_map/put_out/pallas_call | solution.py:512
